TPU v7x, 32 devices: a whole 2x2x4 slice. The times are simulated.
32 devices in a mesh: groups: 2 (over y), pages: 4 (over z), patches: 4 (over x, core).
Axes of the slice: x: 2, y: 2, z: 4, core: 2. Of those that a mesh axis runs over, the one named last changes fastest.
Arguments:
- queries: bfloat16 [16, 32, 128], P(('groups', 'pages'), 'patches'), parts along dimension 0, may hold values from -6 to 6
- gallery: bfloat16 [640, 1024, 128], P(('groups', 'pages'), 'patches'), parts along dimension 0, may hold values from -0.5 to 0.5
- page_rows: int32 [640], P('groups'), parts along dimension 0, may hold values from 0 to 319, as said below
- candidates: int32 [16, 32], P(('groups', 'pages')), parts along dimension 0, may hold values from 0 to 319, as said below
Outputs:
- scores: float32 [16, 32], P(('groups', 'pages')), parts along dimension 0
There are 2 independent parts, one for each index of `groups`. A program takes and returns all parts, laid end to end along the dimension named above; each array names one. Nothing has to cross between parts.
Inputs may be any that keep to these rules, and one draw needn't show every extreme that they name: A permutation: page id c is stored at row page_rows[c] of gallery, which lies on pages index page_rows[c] // 80. Each query's 32 page ids are distinct. The 2 queries of one pages index have at most 48 candidates stored on one pages index, and in every draw some pages index stores exactly 48 candidates of the queries of every pages index.
All inputs are finite; a program needn't handle non-finite values.
Results may differ from a plain program's by a relative error of at most 0.0003.
Values may be sent and summed in bfloat16 or wider, within the bound.
A program may use at most 64 MiB of HBM per device.

v0:
```python
import functools

import jax
import jax.numpy as jnp
from jax import lax
from jax.experimental import pallas as pl
from jax.experimental.pallas import tpu as pltpu
from jax.sharding import PartitionSpec as P

MESH = pl.DeviceIdType.MESH


def up(n, m):
    return -(-n // m) * m


def group_of(n, most):
    return max(d for d in range(1, most + 1) if n % d == 0)


def repeat(n, body):
    if n <= 16:
        for k in range(n):
            body(k)
    else:

        @pl.loop(0, n)
        def _(k):
            body(k)


def to_column(row):
    n = row.shape[1]
    eye = lax.broadcasted_iota(jnp.int32, (n, n), 0) == lax.broadcasted_iota(jnp.int32, (n, n), 1)
    return jnp.sum(jnp.where(eye, row, 0.0), axis=1, keepdims=True)


def to_row(column):
    n = column.shape[0]
    eye = lax.broadcasted_iota(jnp.int32, (n, n), 0) == lax.broadcasted_iota(jnp.int32, (n, n), 1)
    return jnp.sum(jnp.where(eye, column, 0.0), axis=0, keepdims=True)


def top_row(sims):
    rows, width = sims.shape
    chains = 4
    if rows % (8 * chains) == 0:
        sims = jnp.max(sims.reshape(rows // (8 * chains), chains, 8, width), axis=0)
        sims = jnp.maximum(jnp.maximum(sims[0], sims[1]), jnp.maximum(sims[2], sims[3]))
    return jnp.max(sims, axis=0, keepdims=True)


def kernel(
    dims,
    q_hbm,
    g_ref,
    rows_hbm,
    cand_hbm,
    out_ref,
    q_ref,
    rows_ref,
    cand_ref,
    q_all,
    g_buf,
    best,
    best_in,
    send,
    arrived,
    g_sem,
    a_sem,
    q_out,
    q_in,
    b_out,
    b_in,
    s_out,
    s_in,
):
    n_pages, n_patches, nq, tokens = dims
    devices = n_pages * n_patches
    page_count = g_ref.shape[0]
    share = page_count // n_patches
    me_g = lax.axis_index("groups")
    me_p = lax.axis_index("pages")
    me_j = lax.axis_index("patches")
    me = me_p * n_patches + me_j

    def owner(step):
        half = n_patches // 2
        chip, core = me_j // 2, lax.rem(me_j, 2)
        far = n_patches - 1 - step
        return lax.rem(chip + far // 2, half) * 2 + lax.rem(core + far, 2)

    def gallery_copy(step):
        first = owner(step) * share
        return pltpu.make_async_copy(
            g_ref.at[pl.ds(first, share)], g_buf.at[pl.ds(first, share)], g_sem.at[step]
        )

    def peer(k):
        far = devices - 1 - k
        p = lax.rem(me_p + far // n_patches, n_pages)
        j = lax.rem(me_j + far % n_patches, n_patches)
        return p, j

    barrier = pltpu.get_barrier_semaphore()

    def greet(k):
        p, j = peer(k)
        pl.semaphore_signal(barrier, inc=1, device_id=(me_g, p, j), device_id_type=MESH)

    repeat(devices - 1, greet)
    small = [
        pltpu.make_async_copy(source, target, a_sem.at[k])
        for k, (source, target) in enumerate(
            ((q_hbm, q_ref), (cand_hbm, cand_ref), (rows_hbm, rows_ref))
        )
    ]
    for copy in small:
        copy.start()
    for step in range(n_patches):
        gallery_copy(step).start()
    send[...] = jnp.zeros_like(send)
    if best.shape[2] > share:
        spare = best.at[:, :, share:, :]
        spare[...] = jnp.zeros(spare.shape, jnp.float32)
    for copy in small:
        copy.wait()

    q_all[me] = q_ref[...]
    page_rows = rows_ref[...].astype(jnp.float32).reshape(1, -1)
    columns = []
    for q in range(nq):
        wanted = to_column(cand_ref[q : q + 1, :].astype(jnp.float32))
        ids = lax.broadcasted_iota(jnp.int32, (wanted.shape[0], page_rows.shape[1]), 1)
        hit = ids.astype(jnp.float32) == wanted
        columns.append(jnp.sum(jnp.where(hit, page_rows, 0.0), axis=1, keepdims=True))

    pl.semaphore_wait(barrier, devices - 1)

    half_pages = n_pages // 2
    half_devices = devices // 2
    my_half = me_p // half_pages

    def send_queries(k):
        p, j = peer(k)
        pltpu.make_async_remote_copy(
            src_ref=q_ref,
            dst_ref=q_all.at[me],
            send_sem=q_out,
            recv_sem=q_in.at[lax.rem(p // half_pages + my_half, 2)],
            device_id=(me_g, p, j),
            device_id_type=MESH,
        ).start()

    repeat(devices - 1, send_queries)
    rest_q = q_all.at[pl.ds(0, devices - 1)]

    unit = group_of(share, 20)

    def half_weights(half, others):
        some = q_all.at[pl.ds(0, others)]
        pltpu.make_async_copy(some, some, q_in.at[0 if others < half_devices else 1]).wait()
        rows = q_all[pl.ds(half * half_devices, half_devices)]
        rows = rows.reshape(rows.shape[0] * rows.shape[1], rows.shape[2])
        none = jnp.zeros_like(rows)
        return jnp.concatenate(
            [jnp.concatenate([rows, none], axis=1), jnp.concatenate([none, rows], axis=1)], axis=0
        )

    def part_maxima(part, half, weights):
        def block(start):
            for k in range(0, unit, 2):
                first, second = start + k, start + min(k + 1, unit - 1)
                pair = jnp.concatenate(
                    [g_buf[part * share + first], g_buf[part * share + second]], axis=1
                )
                sims = lax.dot_general(
                    pair, weights, (((1,), (1,)), ((), ())), preferred_element_type=jnp.float32
                )
                row = top_row(sims)
                width = row.shape[1] // 2
                best[part, half, pl.ds(first, 1), :] = row[:, :width]
                best[part, half, pl.ds(second, 1), :] = row[:, width:]

        if unit == share:
            block(0)
        else:
            pl.loop(0, share, step=unit)(block)

    def best_copy(step):
        part = owner(step)
        return pltpu.make_async_remote_copy(
            src_ref=best.at[part],
            dst_ref=best_in.at[step],
            send_sem=b_out.at[step],
            recv_sem=b_in.at[step],
            device_id=(me_g, me_p, part),
            device_id_type=MESH,
        )

    for step in range(n_patches):
        gallery_copy(step).wait()
    weights = half_weights(my_half, half_devices - 1)
    for step in range(n_patches):
        part_maxima(owner(step), my_half, weights)
    weights = half_weights(1 - my_half, half_devices)
    for step in range(n_patches):
        part_maxima(owner(step), 1 - my_half, weights)
        if step < n_patches - 1:
            best_copy(step).start()

    width = 2 * best.shape[3]
    own_tokens = tokens // n_patches
    column = lax.broadcasted_iota(jnp.int32, (nq * n_pages, width), 1)
    query = lax.broadcasted_iota(jnp.int32, (nq * n_pages, width), 0)
    position = column // own_tokens
    named = position // (n_patches * nq) * nq + position % nq
    weights = jnp.where(named == query, 1.0 / tokens, 0.0)

    total = best[me_j]
    for step in range(n_patches - 1):
        best_copy(step).wait_recv()
        total = jnp.maximum(total, best_in[step])
    scores = sum(
        lax.dot_general(
            weights[:, half * best.shape[3] : (half + 1) * best.shape[3]],
            total[half],
            (((1,), (1,)), ((), ())),
            precision=lax.Precision.HIGHEST,
            preferred_element_type=jnp.float32,
        )
        for half in range(2)
    )
    for p in range(n_pages):
        send[p, :, : scores.shape[1]] = scores[p * nq : (p + 1) * nq, :]
    arrived[me] = send[me_p]

    def send_scores(k):
        p, j = peer(k)
        pltpu.make_async_remote_copy(
            src_ref=send.at[p],
            dst_ref=arrived.at[me],
            send_sem=s_out,
            recv_sem=s_in,
            device_id=(me_g, p, j),
            device_id_type=MESH,
        ).start()

    repeat(devices - 1, send_scores)
    rest_s = arrived.at[pl.ds(0, devices - 1)]
    pltpu.make_async_copy(rest_s, rest_s, s_in).wait()

    lanes = arrived.shape[2]
    spots = lax.broadcasted_iota(jnp.int32, (cand_ref.shape[1], lanes), 1).astype(jnp.float32)
    for q in range(nq):
        offset = columns[q] - spots

        def add(s, picked):
            first = jnp.float32(s * share) if isinstance(s, int) else (s * share).astype(jnp.float32)
            return picked + jnp.where(offset == first, arrived[s, q : q + 1, :], 0.0)

        picked = jnp.zeros(offset.shape, jnp.float32)
        if devices <= 16:
            for s in range(devices):
                picked = add(s, picked)
        else:
            picked = lax.fori_loop(0, devices, add, picked)
        out_ref[q : q + 1, :] = to_row(jnp.sum(picked, axis=1, keepdims=True))

    pltpu.make_async_copy(rest_q, rest_q, q_out).wait()
    for step in range(n_patches - 1):
        best_copy(step).wait_send()
    pltpu.make_async_copy(rest_s, rest_s, s_out).wait()


def body(queries, gallery, page_rows, candidates):
    nq, own_tokens, dim = queries.shape
    page_count, patches, _ = gallery.shape
    n_pages, n_patches = lax.axis_size("pages"), lax.axis_size("patches")
    devices = n_pages * n_patches
    share = page_count // n_patches
    rows = up(share, 8)
    width = devices * nq * own_tokens
    vmem = pl.BlockSpec(memory_space=pltpu.VMEM)
    dma = pltpu.SemaphoreType.DMA
    return pl.pallas_call(
        functools.partial(kernel, (n_pages, n_patches, nq, own_tokens * n_patches)),
        out_shape=pltpu.VMEM(candidates.shape, jnp.float32),
        in_specs=[pl.BlockSpec(memory_space=pl.ANY)] * 4,
        out_specs=vmem,
        scratch_shapes=[
            pltpu.VMEM((nq * own_tokens, dim), jnp.bfloat16),
            pltpu.VMEM(page_rows.shape, jnp.int32),
            pltpu.VMEM(candidates.shape, jnp.int32),
            pltpu.VMEM((devices, nq * own_tokens, dim), jnp.bfloat16),
            pltpu.VMEM(gallery.shape, jnp.bfloat16),
            pltpu.VMEM((n_patches, 2, rows, width // 2), jnp.float32),
            pltpu.VMEM((n_patches, 2, rows, width // 2), jnp.float32),
            pltpu.VMEM((n_pages, nq, up(rows, 128)), jnp.float32),
            pltpu.VMEM((devices, nq, up(rows, 128)), jnp.float32),
            dma((n_patches,)),
            dma((3,)),
            dma,
            dma((2,)),
            dma((n_patches,)),
            dma((n_patches,)),
            dma,
            dma,
        ],
        compiler_params=pltpu.CompilerParams(collective_id=0, has_side_effects=True),
    )(
        queries.reshape(nq * own_tokens, dim),
        gallery,
        page_rows,
        candidates,
    )


def solution(mesh):
    in_specs = (
        P(("groups", "pages"), "patches", None),
        P(("groups", "pages"), "patches", None),
        P("groups"),
        P(("groups", "pages"), None),
    )
    out_specs = P(("groups", "pages"), None)
    return jax.shard_map(body, mesh=mesh, in_specs=in_specs, out_specs=out_specs, check_vma=False)
```

profile of v0, /device:TPU:0, one launch (start us, length us, event | category | flops | bytes accessed | tf_op | source)
XLA Modules:
  0.0 18.9 jit_solution(11482510503954362007)
XLA Ops:
  0.0 18.4 %shard_map.46 = f32[2,32]{1,0:T(2,128)S(1)} custom-call(bf16[16,128]{1,0:T(8,128)(2,1)} %bitcast.1, bf16[80,256,128]{2,1,0:T(8,128)(2,1)} %g_ref.1, s32[320]{0:T(512)} %rows_hbm.1, s32[2,32]{1,0:T(2,128)} %cand_hbm.1), custom_call_target="tpu_custom_call" | custom-call | tf_op jit(solution)/shard_map/pallas_call | solution.py:286
  18.4 0.6 %copy.6 = f32[2,32]{1,0:T(2,128)} copy(f32[2,32]{1,0:T(2,128)S(1)} %shard_map.46) | data formatting | bytes 512
where the time goes:
time: 19.1 us; the launch traced here: 18.9 us
  Pallas kernels  18.4 us (96%)
  local copies, waits for them, and re-layouts  0.56 us (3%)
    pallas_call x1, Pallas kernels, body(): pl.pallas_call(functools.partial(kernel, (n_pages, n_patches, nq, own_tok...  18.4 us
    unnamed x1, local copies, waits for them, and re-layouts  0.56 us

commit v1 on v0

v1 whole, which is shorter than its diff:
```python
import functools

import jax
import jax.numpy as jnp
from jax import lax
from jax.experimental import pallas as pl
from jax.experimental.pallas import tpu as pltpu
from jax.sharding import PartitionSpec as P

MESH = pl.DeviceIdType.MESH


def up(n, m):
    return -(-n // m) * m


def repeat(n, body):
    if n <= 16:
        for k in range(n):
            body(k)
    else:

        @pl.loop(0, n)
        def _(k):
            body(k)


def to_column(row):
    n = row.shape[1]
    eye = lax.broadcasted_iota(jnp.int32, (n, n), 0) == lax.broadcasted_iota(jnp.int32, (n, n), 1)
    return jnp.sum(jnp.where(eye, row, 0.0), axis=1, keepdims=True)


def to_row(column):
    n = column.shape[0]
    eye = lax.broadcasted_iota(jnp.int32, (n, n), 0) == lax.broadcasted_iota(jnp.int32, (n, n), 1)
    return jnp.sum(jnp.where(eye, column, 0.0), axis=0, keepdims=True)


def top_row(sims):
    rows, width = sims.shape
    chains = 4
    if rows % (8 * chains) == 0:
        sims = jnp.max(sims.reshape(rows // (8 * chains), chains, 8, width), axis=0)
        sims = jnp.maximum(jnp.maximum(sims[0], sims[1]), jnp.maximum(sims[2], sims[3]))
    return jnp.max(sims, axis=0, keepdims=True)


def kernel(
    dims,
    q_hbm,
    g_ref,
    rows_hbm,
    cand_hbm,
    out_ref,
    q_ref,
    rows_ref,
    cand_ref,
    q_all,
    g_buf,
    lists,
    slots,
    best,
    best_in,
    send,
    arrived,
    g_sem,
    a_sem,
    q_out,
    q_in,
    l_own,
    l_out,
    l_in,
    b_out,
    b_in,
    s_out,
    s_in,
):
    n_pages, n_patches, nq, tokens = dims
    devices = n_pages * n_patches
    page_count = g_ref.shape[0]
    pairs = best.shape[1]
    lanes = lists.shape[2]
    me_g = lax.axis_index("groups")
    me_p = lax.axis_index("pages")
    me_j = lax.axis_index("patches")
    finisher = lax.rem(me_j, 2) == 1
    finishers = n_patches // 2

    def there(p, j):
        return (me_g, p, j)

    def holder(k):
        k = jnp.int32(k)
        below = me_p
        above = n_pages - 1 - me_p
        both = 2 * jnp.minimum(below, above)
        longest = jnp.maximum(below, above)
        single = longest - both // 2
        first = jnp.where(below > above, k, n_pages - 1 - k)
        rest = k - single
        alternating = jnp.where(
            lax.rem(rest, 2) == 0, both // 2 - rest // 2, -(both // 2 - rest // 2)
        )
        return jnp.where(k < single, first, me_p + alternating)

    def group(step):
        if isinstance(step, int) and step == 0:
            return me_p
        if isinstance(step, int) and step == 1:
            return jnp.where(me_p > 0, me_p - 1, 1)
        k = step - 2
        return jnp.where(k < me_p - 1, k, k + 2)

    def peer(k):
        if isinstance(k, int):
            p = holder(k // n_patches) if k < devices - n_patches else me_p
            spread = k % n_patches if k < devices - n_patches else k % n_patches + 1
        else:
            far = k < devices - n_patches
            p = jnp.where(far, holder(k // n_patches), me_p)
            spread = jnp.where(far, lax.rem(k, n_patches), lax.rem(k, n_patches) + 1)
        return p, lax.rem(me_j + n_patches - spread, n_patches)

    barrier = pltpu.get_barrier_semaphore()

    def greet(k):
        p, j = peer(k)
        pl.semaphore_signal(barrier, inc=1, device_id=there(p, j), device_id_type=MESH)

    repeat(devices - 1, greet)
    small = [
        pltpu.make_async_copy(source, target, a_sem.at[k])
        for k, (source, target) in enumerate(
            ((q_hbm, q_ref), (cand_hbm, cand_ref), (rows_hbm, rows_ref))
        )
    ]
    for copy in small:
        copy.start()
    gallery_copy = pltpu.make_async_copy(g_ref, g_buf, g_sem)
    gallery_copy.start()
    send[...] = jnp.zeros_like(send)
    for copy in small:
        copy.wait()

    q_all[me_p, me_j] = q_ref[...]
    page_rows = rows_ref[...].astype(jnp.float32).reshape(1, -1)
    columns = []
    for q in range(nq):
        wanted = to_column(cand_ref[q : q + 1, :].astype(jnp.float32))
        ids = lax.broadcasted_iota(jnp.int32, (wanted.shape[0], page_rows.shape[1]), 1)
        hit = ids.astype(jnp.float32) == wanted
        columns.append(jnp.sum(jnp.where(hit, page_rows, 0.0), axis=1, keepdims=True))
    row = jnp.concatenate(columns, axis=0)
    held_by = jnp.zeros_like(row)
    for h in range(1, n_pages):
        held_by = held_by + jnp.where(row >= float(h * page_count), 1.0, 0.0)
    local = row - held_by * float(page_count)
    n = row.shape[0]
    earlier = lax.broadcasted_iota(jnp.int32, (n, n), 1) < lax.broadcasted_iota(jnp.int32, (n, n), 0)
    same = to_row(held_by) == held_by
    place = jnp.sum(jnp.where(earlier & same, 1.0, 0.0), axis=1, keepdims=True)
    key = held_by * float(lanes) + place
    lane = lax.broadcasted_iota(jnp.int32, (n, lanes), 1)

    def make_list(h):
        chosen = key == (lane + h * lanes).astype(jnp.float32)
        found = jnp.sum(jnp.where(chosen, local, 0.0), axis=0, keepdims=True).astype(jnp.int32)
        lists[h] = jnp.clip(found, 0, page_count - 1)

    repeat(n_pages, make_list)
    own_list = pltpu.make_async_copy(lists.at[me_p], slots.at[me_p], l_own)
    own_list.start()

    pl.semaphore_wait(barrier, devices - 1)

    def send_queries(k):
        p, j = peer(k)
        pltpu.make_async_remote_copy(
            src_ref=q_ref,
            dst_ref=q_all.at[me_p, me_j],
            send_sem=q_out,
            recv_sem=q_in.at[me_p],
            device_id=there(p, j),
            device_id_type=MESH,
        ).start()

    def send_list(k):
        p = holder(k)
        pltpu.make_async_remote_copy(
            src_ref=lists.at[p],
            dst_ref=slots.at[me_p],
            send_sem=l_out,
            recv_sem=l_in.at[me_p],
            device_id=there(p, me_j),
            device_id_type=MESH,
        ).start()

    repeat(n_pages - 1, send_list)
    repeat(devices - 1, send_queries)

    def maxima(g):
        rows = q_all[g].reshape(n_patches * q_all.shape[2], q_all.shape[3])
        none = jnp.zeros_like(rows)
        weights = jnp.concatenate(
            [jnp.concatenate([rows, none], axis=1), jnp.concatenate([none, rows], axis=1)], axis=0
        )
        for k in range(pairs):
            pair = jnp.concatenate([g_buf[slots[g, 0, k]], g_buf[slots[g, 0, pairs + k]]], axis=1)
            sims = lax.dot_general(
                pair, weights, (((1,), (1,)), ((), ())), preferred_element_type=jnp.float32
            )
            best[g, k : k + 1, :] = top_row(sims)

    def best_copy(g, j):
        return pltpu.make_async_remote_copy(
            src_ref=best.at[g],
            dst_ref=best_in.at[g, me_j],
            send_sem=b_out,
            recv_sem=b_in.at[g],
            device_id=there(me_p, j),
            device_id_type=MESH,
        )

    def send_best(g):
        for k in range(1, finishers):
            best_copy(g, lax.rem(me_j // 2 + k, finishers) * 2 + 1).start()

        @pl.when(jnp.logical_not(finisher))
        def _():
            best_copy(g, me_j + 1).start()

    width = best.shape[2]
    own_tokens = tokens // n_patches
    column = lax.broadcasted_iota(jnp.int32, (send.shape[1], width), 1)
    query = lax.broadcasted_iota(jnp.int32, (send.shape[1], width), 0)
    position = column // own_tokens
    named = position // (n_patches * nq) * nq + position % nq
    mean = jnp.where(named == query, 1.0 / tokens, 0.0)

    def score_copy(g, k):
        return pltpu.make_async_remote_copy(
            src_ref=send.at[g],
            dst_ref=arrived.at[me_p],
            send_sem=s_out,
            recv_sem=s_in.at[me_p],
            device_id=there(g, me_j - k),
            device_id_type=MESH,
        )

    def finish(step):
        g = group(step)
        others = best_in.at[g, pl.ds(0, n_patches - 1)]
        pltpu.make_async_copy(others, others, b_in.at[g]).wait()
        total = best[g]
        for k in range(1, n_patches):
            total = jnp.maximum(total, best_in[g, lax.rem(me_j + k, n_patches)])
        scores = lax.dot_general(
            mean,
            total,
            (((1,), (1,)), ((), ())),
            precision=lax.Precision.HIGHEST,
            preferred_element_type=jnp.float32,
        )
        send[g, :, :pairs] = scores
        score_copy(g, 1).start()
        if isinstance(step, int) and step == 0:
            arrived[me_p] = send[g]
        else:
            score_copy(g, 0).start()

    def take(step):
        g = group(step)
        if isinstance(step, int) and step == 0:
            some = q_all.at[g, pl.ds(0, n_patches - 1)]
            pltpu.make_async_copy(some, some, q_in.at[g]).wait()
            own_list.wait()
            gallery_copy.wait()
        else:
            some = q_all.at[g]
            pltpu.make_async_copy(some, some, q_in.at[g]).wait()
            pltpu.make_async_copy(slots.at[g], slots.at[g], l_in.at[g]).wait()
        maxima(g)
        send_best(g)

    def maybe_finish(step):
        @pl.when(finisher)
        def _():
            finish(step)

    lag = min(2, n_pages)
    head = min(n_pages, 4)
    for step in range(head):
        take(step)
        if step >= lag:
            maybe_finish(step - lag)
    if head < n_pages:
        for step in range(head - lag, head):
            maybe_finish(step)

        @pl.loop(head, n_pages)
        def _(step):
            take(step)
            maybe_finish(step)

    else:
        for step in range(n_pages - lag, n_pages):
            maybe_finish(step)

    spots = lax.broadcasted_iota(jnp.int32, (cand_ref.shape[1], lanes), 1)
    cands = cand_ref.shape[1]

    def pick(h, picked):
        found = []
        for q in range(nq):
            mine = key[q * cands : (q + 1) * cands]
            total = picked[q]
            for half in range(2):
                spot = (spots + (h * lanes + half * pairs)).astype(jnp.float32)
                hit = (mine == spot) & (spots < pairs)
                total = total + jnp.where(hit, arrived[h, half * nq + q : half * nq + q + 1, :], 0.0)
            found.append(total)
        return tuple(found)

    def wait_scores(h):
        pltpu.make_async_copy(arrived.at[h], arrived.at[h], s_in.at[h]).wait()

    @pl.when(jnp.logical_not(finisher))
    def _():
        wait_scores(me_p)

    picked = tuple(jnp.zeros((cands, lanes), jnp.float32) for _ in range(nq))
    picked = pick(me_p, picked)
    if n_pages <= 16:
        for k in reversed(range(n_pages - 1)):
            wait_scores(holder(k))
            picked = pick(holder(k), picked)
    else:

        def later(k, picked):
            wait_scores(holder(k))
            return pick(holder(k), picked)

        picked = lax.fori_loop(0, n_pages - 1, later, picked)
    for q in range(nq):
        out_ref[q : q + 1, :] = to_row(jnp.sum(picked[q], axis=1, keepdims=True))

    def drain(k):
        pltpu.make_async_copy(q_ref, q_ref, q_out).wait()

    rest = q_all.at[pl.ds(0, n_pages - 1)]
    pltpu.make_async_copy(rest, rest, q_out).wait()
    rest = q_all.at[0, pl.ds(0, n_patches - 1)]
    pltpu.make_async_copy(rest, rest, q_out).wait()
    rest = lists.at[pl.ds(0, n_pages - 1)]
    pltpu.make_async_copy(rest, rest, l_out).wait()
    if finishers > 1:
        rest = best_in.at[:, pl.ds(0, finishers - 1)]
        pltpu.make_async_copy(rest, rest, b_out).wait()

    @pl.when(jnp.logical_not(finisher))
    def _():
        pltpu.make_async_copy(best, best, b_out).wait()

    @pl.when(finisher)
    def _():
        pltpu.make_async_copy(arrived, arrived, s_out).wait()
        rest = arrived.at[pl.ds(0, n_pages - 1)]
        pltpu.make_async_copy(rest, rest, s_out).wait()


def body(queries, gallery, page_rows, candidates):
    nq, own_tokens, dim = queries.shape
    n_pages, n_patches = lax.axis_size("pages"), lax.axis_size("patches")
    most = 3 * nq * candidates.shape[1] // n_pages
    pairs = up(up(most, 2) // 2, 8)
    lanes = up(2 * pairs, 128)
    width = 2 * n_patches * nq * own_tokens
    vmem = pl.BlockSpec(memory_space=pltpu.VMEM)
    dma = pltpu.SemaphoreType.DMA
    return pl.pallas_call(
        functools.partial(kernel, (n_pages, n_patches, nq, own_tokens * n_patches)),
        out_shape=pltpu.VMEM(candidates.shape, jnp.float32),
        in_specs=[pl.BlockSpec(memory_space=pl.ANY)] * 4,
        out_specs=vmem,
        scratch_shapes=[
            pltpu.VMEM((nq * own_tokens, dim), jnp.bfloat16),
            pltpu.VMEM(page_rows.shape, jnp.int32),
            pltpu.VMEM(candidates.shape, jnp.int32),
            pltpu.VMEM((n_pages, n_patches, nq * own_tokens, dim), jnp.bfloat16),
            pltpu.VMEM(gallery.shape, jnp.bfloat16),
            pltpu.VMEM((n_pages, 1, lanes), jnp.int32),
            pltpu.SMEM((n_pages, 1, lanes), jnp.int32),
            pltpu.VMEM((n_pages, pairs, width), jnp.float32),
            pltpu.VMEM((n_pages, n_patches, pairs, width), jnp.float32),
            pltpu.VMEM((n_pages, up(2 * nq, 8), lanes), jnp.float32),
            pltpu.VMEM((n_pages, up(2 * nq, 8), lanes), jnp.float32),
            dma,
            dma((3,)),
            dma,
            dma((n_pages,)),
            dma,
            dma,
            dma((n_pages,)),
            dma,
            dma((n_pages,)),
            dma,
            dma((n_pages,)),
        ],
        compiler_params=pltpu.CompilerParams(collective_id=0, has_side_effects=True),
    )(
        queries.reshape(nq * own_tokens, dim),
        gallery,
        page_rows,
        candidates,
    )


def solution(mesh):
    in_specs = (
        P(("groups", "pages"), "patches", None),
        P(("groups", "pages"), "patches", None),
        P("groups"),
        P(("groups", "pages"), None),
    )
    out_specs = P(("groups", "pages"), None)
    return jax.shard_map(body, mesh=mesh, in_specs=in_specs, out_specs=out_specs, check_vma=False)
```

time: 19.1 us -> 17.6 us (0.921)
  Pallas kernels: 18.4 us -> 16.8 us
    pallas_call x1, Pallas kernels: 18.4 us -> 16.8 us  [body(): pl.pallas_call(functools.partial(kernel, (n_pages, n_patches, nq, own_tok...]
where the time goes in v1:
time: 17.6 us; the launch traced here: 17.4 us
  Pallas kernels  16.8 us (95%)
  local copies, waits for them, and re-layouts  0.56 us (3%)
    pallas_call x1, Pallas kernels, body(): pl.pallas_call(functools.partial(kernel, (n_pages, n_patches, nq, own_tok...  16.8 us
    unnamed x1, local copies, waits for them, and re-layouts  0.56 us

profile of v1, /device:TPU:0, one launch (start us, length us, event | category | flops | bytes accessed | tf_op | source)
XLA Modules:
  0.0 17.4 jit_solution(155335743188382212)
XLA Ops:
  0.0 16.8 %shard_map.46 = f32[2,32]{1,0:T(2,128)S(1)} custom-call(bf16[16,128]{1,0:T(8,128)(2,1)} %bitcast.1, bf16[80,256,128]{2,1,0:T(8,128)(2,1)} %g_ref.1, s32[320]{0:T(512)} %rows_hbm.1, s32[2,32]{1,0:T(2,128)} %cand_hbm.1), custom_call_target="tpu_custom_call" | custom-call | tf_op jit(solution)/shard_map/pallas_call | solution.py:381
  16.9 0.6 %copy.6 = f32[2,32]{1,0:T(2,128)} copy(f32[2,32]{1,0:T(2,128)S(1)} %shard_map.46) | data formatting | bytes 512

commit v2 on v1

--- a/solution.py
+++ b/solution.py
@@ -62,6 +62,7 @@
     slots,
     best,
     best_in,
+    direct_in,
     send,
     arrived,
     g_sem,
@@ -75,6 +76,9 @@
     b_in,
     s_out,
     s_in,
+    d_out,
+    d_in,
+    ready,
 ):
     n_pages, n_patches, nq, tokens = dims
     devices = n_pages * n_patches
@@ -86,6 +90,7 @@
     me_j = lax.axis_index("patches")
     finisher = lax.rem(me_j, 2) == 1
     finishers = n_patches // 2
+    direct = (me_p == 0) & (me_j < 2)
 
     def there(p, j):
         return (me_g, p, j)
@@ -105,30 +110,38 @@
         return jnp.where(k < single, first, me_p + alternating)
 
     def group(step):
-        if isinstance(step, int) and step == 0:
-            return me_p
-        if isinstance(step, int) and step == 1:
-            return jnp.where(me_p > 0, me_p - 1, 1)
-        k = step - 2
-        return jnp.where(k < me_p - 1, k, k + 2)
-
-    def peer(k):
-        if isinstance(k, int):
-            p = holder(k // n_patches) if k < devices - n_patches else me_p
-            spread = k % n_patches if k < devices - n_patches else k % n_patches + 1
-        else:
-            far = k < devices - n_patches
-            p = jnp.where(far, holder(k // n_patches), me_p)
-            spread = jnp.where(far, lax.rem(k, n_patches), lax.rem(k, n_patches) + 1)
-        return p, lax.rem(me_j + n_patches - spread, n_patches)
+        step = jnp.int32(step)
+        low = jnp.where(step == 0, me_p, jnp.where(step <= me_p, step - 1, step))
+        high = jnp.where(step < me_p, me_p - 1 - step, jnp.where(step == n_pages - 1, me_p, step + 1))
+        return jnp.where(me_p > 2, high, low)
 
     barrier = pltpu.get_barrier_semaphore()
 
-    def greet(k):
-        p, j = peer(k)
+    def greet(p, j):
         pl.semaphore_signal(barrier, inc=1, device_id=there(p, j), device_id_type=MESH)
 
-    repeat(devices - 1, greet)
+    def across(p, first, act):
+        for k in range(first, n_patches):
+            act(p, lax.rem(me_j + k, n_patches))
+
+    def above(act):
+        def one(k):
+            @pl.when(n_pages - 1 - k > me_p)
+            def _():
+                act(n_pages - 1 - k)
+
+        repeat(n_pages - 1, one)
+
+    def below(act):
+        def one(k):
+            @pl.when(k < me_p)
+            def _():
+                act(k)
+
+        repeat(n_pages - 1, one)
+
+    across(me_p, 1, greet)
+    above(lambda p: across(p, 0, greet))
     small = [
         pltpu.make_async_copy(source, target, a_sem.at[k])
         for k, (source, target) in enumerate(
@@ -172,10 +185,19 @@
     own_list = pltpu.make_async_copy(lists.at[me_p], slots.at[me_p], l_own)
     own_list.start()
 
-    pl.semaphore_wait(barrier, devices - 1)
-
-    def send_queries(k):
-        p, j = peer(k)
+    pl.semaphore_wait(barrier, n_patches - 1 + n_patches * me_p)
+
+    def announce(p):
+        for k in range(2):
+            pl.semaphore_signal(
+                ready.at[me_p], inc=1, device_id=there(p, me_j - k), device_id_type=MESH
+            )
+
+    @pl.when(finisher)
+    def _():
+        below(announce)
+
+    def send_queries(p, j):
         pltpu.make_async_remote_copy(
             src_ref=q_ref,
             dst_ref=q_all.at[me_p, me_j],
@@ -185,8 +207,8 @@
             device_id_type=MESH,
         ).start()
 
-    def send_list(k):
-        p = holder(k)
+    def send_to(p):
+        across(p, 0, send_queries)
         pltpu.make_async_remote_copy(
             src_ref=lists.at[p],
             dst_ref=slots.at[me_p],
@@ -196,8 +218,16 @@
             device_id_type=MESH,
         ).start()
 
-    repeat(n_pages - 1, send_list)
-    repeat(devices - 1, send_queries)
+    across(me_p, 1, send_queries)
+    below(send_to)
+
+    def send_above(k):
+        @pl.when(k + 1 > me_p)
+        def _():
+            pl.semaphore_wait(ready.at[k + 1], 1)
+            send_to(k + 1)
+
+    repeat(n_pages - 1, send_above)
 
     def maxima(g):
         rows = q_all[g].reshape(n_patches * q_all.shape[2], q_all.shape[3])
@@ -222,13 +252,29 @@
             device_id_type=MESH,
         )
 
+    def direct_copy(j):
+        return pltpu.make_async_remote_copy(
+            src_ref=best.at[0],
+            dst_ref=direct_in.at[me_p, me_j],
+            send_sem=d_out,
+            recv_sem=d_in.at[me_p],
+            device_id=there(0, j),
+            device_id_type=MESH,
+        )
+
     def send_best(g):
-        for k in range(1, finishers):
-            best_copy(g, lax.rem(me_j // 2 + k, finishers) * 2 + 1).start()
-
-        @pl.when(jnp.logical_not(finisher))
-        def _():
-            best_copy(g, me_j + 1).start()
+        for j in range(2):
+
+            @pl.when((g == 0) & jnp.logical_not((me_p == 0) & (me_j == j)))
+            def _():
+                direct_copy(j).start()
+
+        for k in range(finishers):
+            j = lax.rem(me_j // 2 + k, finishers) * 2 + 1
+
+            @pl.when((j != me_j) & jnp.logical_not((g == 0) & (j == 1)))
+            def _():
+                best_copy(g, j).start()
 
     width = best.shape[2]
     own_tokens = tokens // n_patches
@@ -248,6 +294,15 @@
             device_id_type=MESH,
         )
 
+    def mean_of(total):
+        return lax.dot_general(
+            mean,
+            total,
+            (((1,), (1,)), ((), ())),
+            precision=lax.Precision.HIGHEST,
+            preferred_element_type=jnp.float32,
+        )
+
     def finish(step):
         g = group(step)
         others = best_in.at[g, pl.ds(0, n_patches - 1)]
@@ -255,118 +310,198 @@
         total = best[g]
         for k in range(1, n_patches):
             total = jnp.maximum(total, best_in[g, lax.rem(me_j + k, n_patches)])
-        scores = lax.dot_general(
-            mean,
-            total,
-            (((1,), (1,)), ((), ())),
-            precision=lax.Precision.HIGHEST,
-            preferred_element_type=jnp.float32,
-        )
-        send[g, :, :pairs] = scores
+        send[g, :, :pairs] = mean_of(total)
         score_copy(g, 1).start()
-        if isinstance(step, int) and step == 0:
+
+        @pl.when(g == me_p)
+        def _():
             arrived[me_p] = send[g]
-        else:
+
+        @pl.when(g != me_p)
+        def _():
             score_copy(g, 0).start()
 
     def take(step):
         g = group(step)
-        if isinstance(step, int) and step == 0:
+
+        @pl.when(g == me_p)
+        def _():
             some = q_all.at[g, pl.ds(0, n_patches - 1)]
             pltpu.make_async_copy(some, some, q_in.at[g]).wait()
             own_list.wait()
-            gallery_copy.wait()
-        else:
+
+        @pl.when(g != me_p)
+        def _():
             some = q_all.at[g]
             pltpu.make_async_copy(some, some, q_in.at[g]).wait()
             pltpu.make_async_copy(slots.at[g], slots.at[g], l_in.at[g]).wait()
+
         maxima(g)
         send_best(g)
 
     def maybe_finish(step):
-        @pl.when(finisher)
+        @pl.when(finisher & jnp.logical_not((me_j == 1) & (group(step) == 0)))
         def _():
             finish(step)
 
-    lag = min(2, n_pages)
-    head = min(n_pages, 4)
-    for step in range(head):
-        take(step)
-        if step >= lag:
-            maybe_finish(step - lag)
-    if head < n_pages:
-        for step in range(head - lag, head):
+    gallery_copy.wait()
+    last = n_pages - 1
+    if n_pages <= 4:
+        for step in range(n_pages):
+            take(step)
+            if step >= 2:
+                maybe_finish(step - 2)
+        for step in range(max(n_pages - 2, 0), n_pages):
             maybe_finish(step)
-
-        @pl.loop(head, n_pages)
+    else:
+
+        @pl.loop(0, last)
         def _(step):
             take(step)
             maybe_finish(step)
 
-    else:
-        for step in range(n_pages - lag, n_pages):
-            maybe_finish(step)
-
-    spots = lax.broadcasted_iota(jnp.int32, (cand_ref.shape[1], lanes), 1)
+        take(last)
+        maybe_finish(last)
+
+    def wait(units, sem):
+        pltpu.make_async_copy(units, units, sem).wait()
+
+    def drain_maxima():
+        wait(q_all.at[pl.ds(0, n_pages - 1)], q_out)
+        wait(q_all.at[0, pl.ds(0, n_patches - 1)], q_out)
+        wait(lists.at[pl.ds(0, n_pages - 1)], l_out)
+
+        def wait_best(full, last):
+            if full > 0:
+                wait(best_in.at[pl.ds(0, n_pages - 1), pl.ds(0, full)], b_out)
+            if last > 0:
+                wait(best_in.at[0, pl.ds(0, last)], b_out)
+
+        @pl.when(jnp.logical_not(finisher))
+        def _():
+            wait_best(finishers, finishers - 1)
+
+        @pl.when(me_j == 1)
+        def _():
+            wait_best(finishers - 1, finishers - 1)
+
+        @pl.when(finisher & (me_j > 1))
+        def _():
+            wait_best(finishers - 1, finishers - 2)
+
+        wait(best.at[0], d_out)
+
+        @pl.when(jnp.logical_not(direct))
+        def _():
+            wait(best.at[0], d_out)
+
+    def drain_scores():
+        @pl.when(me_j == 1)
+        def _():
+            wait(send.at[pl.ds(0, n_pages - 1)], s_out)
+
+            @pl.when(me_p > 0)
+            def _():
+                wait(send.at[pl.ds(0, n_pages - 2)], s_out)
+
+            @pl.when(me_p == 0)
+            def _():
+                wait(send.at[pl.ds(0, n_pages - 1)], s_out)
+
+        @pl.when(finisher & (me_j > 1))
+        def _():
+            wait(send.at[pl.ds(0, n_pages)], s_out)
+            wait(send.at[pl.ds(0, n_pages - 1)], s_out)
+
+    drain_maxima()
     cands = cand_ref.shape[1]
-
-    def pick(h, picked):
+    spots = lax.broadcasted_iota(jnp.int32, (cands, pairs), 1)
+    zeros = tuple(jnp.zeros((cands, pairs), jnp.float32) for _ in range(nq))
+
+    def pick(h, scores, picked):
         found = []
         for q in range(nq):
             mine = key[q * cands : (q + 1) * cands]
             total = picked[q]
             for half in range(2):
                 spot = (spots + (h * lanes + half * pairs)).astype(jnp.float32)
-                hit = (mine == spot) & (spots < pairs)
-                total = total + jnp.where(hit, arrived[h, half * nq + q : half * nq + q + 1, :], 0.0)
+                line = scores[half * nq + q : half * nq + q + 1, :]
+                total = total + jnp.where(mine == spot, line, 0.0)
             found.append(total)
         return tuple(found)
 
-    def wait_scores(h):
-        pltpu.make_async_copy(arrived.at[h], arrived.at[h], s_in.at[h]).wait()
-
-    @pl.when(jnp.logical_not(finisher))
+    def put(picked):
+        for q in range(nq):
+            out_ref[q : q + 1, :] = to_row(jnp.sum(picked[q], axis=1, keepdims=True))
+
+    def over_others(step, picked):
+        if n_pages <= 16:
+            for k in range(n_pages - 1):
+                picked = step(k, picked)
+            return picked
+        return lax.fori_loop(0, n_pages - 1, step, picked)
+
+    @pl.when(direct)
     def _():
-        wait_scores(me_p)
-
-    picked = tuple(jnp.zeros((cands, lanes), jnp.float32) for _ in range(nq))
-    picked = pick(me_p, picked)
-    if n_pages <= 16:
-        for k in reversed(range(n_pages - 1)):
-            wait_scores(holder(k))
-            picked = pick(holder(k), picked)
-    else:
+        key_rows = [to_row(key[q * cands : (q + 1) * cands]) for q in range(nq)]
+        slot = lax.broadcasted_iota(jnp.int32, (pairs, cands), 0)
+        lane_of = lax.broadcasted_iota(jnp.int32, (pairs, width), 1) // own_tokens
+        kind = lane_of // (n_patches * nq) * nq + lane_of % nq
+
+        def hits(h):
+            return [
+                (slot + (h * lanes + half * pairs)).astype(jnp.float32) == key_rows[q]
+                for half in range(2)
+                for q in range(nq)
+            ]
+
+        def add(hit, total, sums):
+            sums = list(sums)
+            for k in range(2 * nq):
+                score = jnp.sum(jnp.where(kind == k, total, 0.0), axis=1, keepdims=True)
+                sums[k % nq] = sums[k % nq] + jnp.where(hit[k], score, 0.0)
+            return tuple(sums)
+
+        sums = tuple(jnp.zeros((pairs, cands), jnp.float32) for _ in range(nq))
+        wait(direct_in.at[0, pl.ds(0, n_patches - 1)], d_in.at[0])
+        total = best[0]
+        for k in range(1, n_patches):
+            total = jnp.maximum(total, direct_in[0, lax.rem(me_j + k, n_patches)])
+        sums = add(hits(0), total, sums)
+
+        def later(k, sums):
+            h = k + 1
+            hit = hits(h)
+            wait(direct_in.at[h], d_in.at[h])
+            total = direct_in[h, 0]
+            for j in range(1, n_patches):
+                total = jnp.maximum(total, direct_in[h, j])
+            return add(hit, total, sums)
+
+        sums = over_others(later, sums)
+        for q in range(nq):
+            out_ref[q : q + 1, :] = jnp.sum(sums[q], axis=0, keepdims=True) * (1.0 / tokens)
+
+    @pl.when(jnp.logical_not(direct))
+    def _():
+        def wait_scores(h):
+            pltpu.make_async_copy(arrived.at[h], arrived.at[h], s_in.at[h]).wait()
+
+        @pl.when(jnp.logical_not(finisher))
+        def _():
+            wait_scores(me_p)
+
+        def scores_of(h):
+            return arrived[h, :, :pairs]
 
         def later(k, picked):
-            wait_scores(holder(k))
-            return pick(holder(k), picked)
-
-        picked = lax.fori_loop(0, n_pages - 1, later, picked)
-    for q in range(nq):
-        out_ref[q : q + 1, :] = to_row(jnp.sum(picked[q], axis=1, keepdims=True))
-
-    def drain(k):
-        pltpu.make_async_copy(q_ref, q_ref, q_out).wait()
-
-    rest = q_all.at[pl.ds(0, n_pages - 1)]
-    pltpu.make_async_copy(rest, rest, q_out).wait()
-    rest = q_all.at[0, pl.ds(0, n_patches - 1)]
-    pltpu.make_async_copy(rest, rest, q_out).wait()
-    rest = lists.at[pl.ds(0, n_pages - 1)]
-    pltpu.make_async_copy(rest, rest, l_out).wait()
-    if finishers > 1:
-        rest = best_in.at[:, pl.ds(0, finishers - 1)]
-        pltpu.make_async_copy(rest, rest, b_out).wait()
-
-    @pl.when(jnp.logical_not(finisher))
-    def _():
-        pltpu.make_async_copy(best, best, b_out).wait()
-
-    @pl.when(finisher)
-    def _():
-        pltpu.make_async_copy(arrived, arrived, s_out).wait()
-        rest = arrived.at[pl.ds(0, n_pages - 1)]
-        pltpu.make_async_copy(rest, rest, s_out).wait()
+            h = holder(n_pages - 2 - k)
+            wait_scores(h)
+            return pick(h, scores_of(h), picked)
+
+        put(over_others(later, pick(me_p, scores_of(me_p), zeros)))
+
+    drain_scores()
 
 
 def body(queries, gallery, page_rows, candidates):
@@ -393,6 +528,7 @@
             pltpu.SMEM((n_pages, 1, lanes), jnp.int32),
             pltpu.VMEM((n_pages, pairs, width), jnp.float32),
             pltpu.VMEM((n_pages, n_patches, pairs, width), jnp.float32),
+            pltpu.VMEM((n_pages, n_patches, pairs, width), jnp.float32),
             pltpu.VMEM((n_pages, up(2 * nq, 8), lanes), jnp.float32),
             pltpu.VMEM((n_pages, up(2 * nq, 8), lanes), jnp.float32),
             dma,
@@ -406,6 +542,9 @@
             dma((n_pages,)),
             dma,
             dma((n_pages,)),
+            dma,
+            dma((n_pages,)),
+            pltpu.SemaphoreType.REGULAR((n_pages,)),
         ],
         compiler_params=pltpu.CompilerParams(collective_id=0, has_side_effects=True),
     )(

time: 17.6 us -> 16.7 us (0.949)
  Pallas kernels: 16.8 us -> 16 us
    pallas_call x1, Pallas kernels: 16.8 us -> 16 us  [body(): pl.pallas_call(functools.partial(kernel, (n_pages, n_patches, nq, own_tok...]
where the time goes in v2:
time: 16.7 us; the launch traced here: 16.5 us
  Pallas kernels  16 us (96%)
  local copies, waits for them, and re-layouts  0.56 us (3%)
    pallas_call x1, Pallas kernels, body(): pl.pallas_call(functools.partial(kernel, (n_pages, n_patches, nq, own_tok...  16 us
    unnamed x1, local copies, waits for them, and re-layouts  0.56 us

profile of v2, /device:TPU:0, one launch (start us, length us, event | category | flops | bytes accessed | tf_op | source)
XLA Modules:
  0.0 16.5 jit_solution(13933564044901201345)
XLA Ops:
  0.0 16.0 %shard_map.46 = f32[2,32]{1,0:T(2,128)S(1)} custom-call(bf16[16,128]{1,0:T(8,128)(2,1)} %bitcast.1, bf16[80,256,128]{2,1,0:T(8,128)(2,1)} %g_ref.1, s32[320]{0:T(512)} %rows_hbm.1, s32[2,32]{1,0:T(2,128)} %cand_hbm.1), custom_call_target="tpu_custom_call" | custom-call | tf_op jit(solution)/shard_map/pallas_call | solution.py:516
  16.0 0.6 %copy.6 = f32[2,32]{1,0:T(2,128)} copy(f32[2,32]{1,0:T(2,128)S(1)} %shard_map.46) | data formatting | bytes 512

commit v3 on v2

--- a/solution.py
+++ b/solution.py
@@ -111,9 +111,10 @@
 
     def group(step):
         step = jnp.int32(step)
-        low = jnp.where(step == 0, me_p, jnp.where(step <= me_p, step - 1, step))
-        high = jnp.where(step < me_p, me_p - 1 - step, jnp.where(step == n_pages - 1, me_p, step + 1))
-        return jnp.where(me_p > 2, high, low)
+        low = jnp.where(step <= me_p, step - 1, step)
+        high = jnp.where(step < me_p, me_p - 1 - step, step)
+        high = jnp.where(step == me_p, me_p - 1, high)
+        return jnp.where(step == 0, me_p, jnp.where(me_p > 2, high, low))
 
     barrier = pltpu.get_barrier_semaphore()
 
@@ -153,10 +154,35 @@
     gallery_copy = pltpu.make_async_copy(g_ref, g_buf, g_sem)
     gallery_copy.start()
     send[...] = jnp.zeros_like(send)
+    pl.semaphore_wait(barrier, n_patches - 1 + n_patches * me_p)
+
+    def announce(p):
+        for k in range(2):
+            pl.semaphore_signal(
+                ready.at[me_p], inc=1, device_id=there(p, me_j - k), device_id_type=MESH
+            )
+
+    @pl.when(finisher)
+    def _():
+        below(announce)
+
     for copy in small:
         copy.wait()
 
     q_all[me_p, me_j] = q_ref[...]
+    def send_queries(p, j):
+        pltpu.make_async_remote_copy(
+            src_ref=q_ref,
+            dst_ref=q_all.at[me_p, me_j],
+            send_sem=q_out,
+            recv_sem=q_in.at[me_p],
+            device_id=there(p, j),
+            device_id_type=MESH,
+        ).start()
+
+    across(me_p, 1, send_queries)
+    below(lambda p: across(p, 0, send_queries))
+
     page_rows = rows_ref[...].astype(jnp.float32).reshape(1, -1)
     columns = []
     for q in range(nq):
@@ -185,30 +211,7 @@
     own_list = pltpu.make_async_copy(lists.at[me_p], slots.at[me_p], l_own)
     own_list.start()
 
-    pl.semaphore_wait(barrier, n_patches - 1 + n_patches * me_p)
-
-    def announce(p):
-        for k in range(2):
-            pl.semaphore_signal(
-                ready.at[me_p], inc=1, device_id=there(p, me_j - k), device_id_type=MESH
-            )
-
-    @pl.when(finisher)
-    def _():
-        below(announce)
-
-    def send_queries(p, j):
-        pltpu.make_async_remote_copy(
-            src_ref=q_ref,
-            dst_ref=q_all.at[me_p, me_j],
-            send_sem=q_out,
-            recv_sem=q_in.at[me_p],
-            device_id=there(p, j),
-            device_id_type=MESH,
-        ).start()
-
-    def send_to(p):
-        across(p, 0, send_queries)
+    def send_list(p):
         pltpu.make_async_remote_copy(
             src_ref=lists.at[p],
             dst_ref=slots.at[me_p],
@@ -218,14 +221,15 @@
             device_id_type=MESH,
         ).start()
 
-    across(me_p, 1, send_queries)
-    below(send_to)
+    below(send_list)
 
     def send_above(k):
         @pl.when(k + 1 > me_p)
         def _():
             pl.semaphore_wait(ready.at[k + 1], 1)
-            send_to(k + 1)
+            for spread in reversed(range(n_patches)):
+                send_queries(k + 1, lax.rem(me_j + spread, n_patches))
+            send_list(k + 1)
 
     repeat(n_pages - 1, send_above)
 
@@ -441,6 +445,25 @@
             return picked
         return lax.fori_loop(0, n_pages - 1, step, picked)
 
+    @pl.when(jnp.logical_not(direct))
+    def _():
+        def wait_scores(h):
+            pltpu.make_async_copy(arrived.at[h], arrived.at[h], s_in.at[h]).wait()
+
+        @pl.when(jnp.logical_not(finisher))
+        def _():
+            wait_scores(me_p)
+
+        def scores_of(h):
+            return arrived[h, :, :pairs]
+
+        def later(k, picked):
+            h = holder(n_pages - 2 - k)
+            wait_scores(h)
+            return pick(h, scores_of(h), picked)
+
+        put(over_others(later, pick(me_p, scores_of(me_p), zeros)))
+
     @pl.when(direct)
     def _():
         key_rows = [to_row(key[q * cands : (q + 1) * cands]) for q in range(nq)]
@@ -481,25 +504,6 @@
         sums = over_others(later, sums)
         for q in range(nq):
             out_ref[q : q + 1, :] = jnp.sum(sums[q], axis=0, keepdims=True) * (1.0 / tokens)
-
-    @pl.when(jnp.logical_not(direct))
-    def _():
-        def wait_scores(h):
-            pltpu.make_async_copy(arrived.at[h], arrived.at[h], s_in.at[h]).wait()
-
-        @pl.when(jnp.logical_not(finisher))
-        def _():
-            wait_scores(me_p)
-
-        def scores_of(h):
-            return arrived[h, :, :pairs]
-
-        def later(k, picked):
-            h = holder(n_pages - 2 - k)
-            wait_scores(h)
-            return pick(h, scores_of(h), picked)
-
-        put(over_others(later, pick(me_p, scores_of(me_p), zeros)))
 
     drain_scores()
 

time: 16.7 us -> 16.6 us (level)
  no operation moved by 1% of the time
where the time goes in v3:
time: 16.6 us; the launch traced here: 16.4 us
  Pallas kernels  15.9 us (96%)
  local copies, waits for them, and re-layouts  0.56 us (3%)
    pallas_call x1, Pallas kernels, body(): pl.pallas_call(functools.partial(kernel, (n_pages, n_patches, nq, own_tok...  15.9 us
    unnamed x1, local copies, waits for them, and re-layouts  0.56 us

profile of v3, /device:TPU:0, one launch (start us, length us, event | category | flops | bytes accessed | tf_op | source)
XLA Modules:
  0.0 16.4 jit_solution(6338913649110760340)
XLA Ops:
  0.0 15.9 %shard_map.46 = f32[2,32]{1,0:T(2,128)S(1)} custom-call(bf16[16,128]{1,0:T(8,128)(2,1)} %bitcast.1, bf16[80,256,128]{2,1,0:T(8,128)(2,1)} %g_ref.1, s32[320]{0:T(512)} %rows_hbm.1, s32[2,32]{1,0:T(2,128)} %cand_hbm.1), custom_call_target="tpu_custom_call" | custom-call | tf_op jit(solution)/shard_map/pallas_call | solution.py:520
  15.9 0.6 %copy.6 = f32[2,32]{1,0:T(2,128)} copy(f32[2,32]{1,0:T(2,128)S(1)} %shard_map.46) | data formatting | bytes 512

commit v4 on v3

--- a/solution.py
+++ b/solution.py
@@ -83,8 +83,10 @@
     n_pages, n_patches, nq, tokens = dims
     devices = n_pages * n_patches
     page_count = g_ref.shape[0]
-    pairs = best.shape[1]
+    packed = best.shape[1]
+    pairs = packed * nq
     lanes = lists.shape[2]
+    own_tokens = tokens // n_patches
     me_g = lax.axis_index("groups")
     me_p = lax.axis_index("pages")
     me_j = lax.axis_index("patches")
@@ -196,6 +198,10 @@
         held_by = held_by + jnp.where(row >= float(h * page_count), 1.0, 0.0)
     local = row - held_by * float(page_count)
     n = row.shape[0]
+    asker = jnp.concatenate(
+        [jnp.full_like(columns[q], float(q)) for q in range(nq)], axis=0
+    )
+    entry = local * float(nq) + asker
     earlier = lax.broadcasted_iota(jnp.int32, (n, n), 1) < lax.broadcasted_iota(jnp.int32, (n, n), 0)
     same = to_row(held_by) == held_by
     place = jnp.sum(jnp.where(earlier & same, 1.0, 0.0), axis=1, keepdims=True)
@@ -204,8 +210,8 @@
 
     def make_list(h):
         chosen = key == (lane + h * lanes).astype(jnp.float32)
-        found = jnp.sum(jnp.where(chosen, local, 0.0), axis=0, keepdims=True).astype(jnp.int32)
-        lists[h] = jnp.clip(found, 0, page_count - 1)
+        found = jnp.sum(jnp.where(chosen, entry, 0.0), axis=0, keepdims=True).astype(jnp.int32)
+        lists[h] = jnp.clip(found, 0, page_count * nq - 1)
 
     repeat(n_pages, make_list)
     own_list = pltpu.make_async_copy(lists.at[me_p], slots.at[me_p], l_own)
@@ -239,12 +245,27 @@
         weights = jnp.concatenate(
             [jnp.concatenate([rows, none], axis=1), jnp.concatenate([none, rows], axis=1)], axis=0
         )
-        for k in range(pairs):
-            pair = jnp.concatenate([g_buf[slots[g, 0, k]], g_buf[slots[g, 0, pairs + k]]], axis=1)
-            sims = lax.dot_general(
-                pair, weights, (((1,), (1,)), ((), ())), preferred_element_type=jnp.float32
-            )
-            best[g, k : k + 1, :] = top_row(sims)
+        lanes_of = lax.broadcasted_iota(jnp.int32, (1, best.shape[2]), 1)
+        place_of = lanes_of // own_tokens % nq
+        for r in range(packed):
+            together = None
+            for i in range(nq):
+                k = i * packed + r
+                ids = [slots[g, 0, k], slots[g, 0, pairs + k]]
+                pair = jnp.concatenate([g_buf[lax.div(v, nq)] for v in ids], axis=1)
+                sims = lax.dot_general(
+                    pair, weights, (((1,), (1,)), ((), ())), preferred_element_type=jnp.float32
+                )
+                tops = top_row(sims)
+                askers = [lax.rem(v, nq) for v in ids]
+                asked = jnp.where(lanes_of < best.shape[2] // 2, askers[0], askers[1])
+                here = tops
+                for q in range(nq):
+                    if q != i:
+                        shift = (i - q) * own_tokens % best.shape[2]
+                        here = jnp.where(asked == q, pltpu.roll(tops, shift, 1), here)
+                together = here if i == 0 else jnp.where(place_of == i, here, together)
+            best[g, r : r + 1, :] = together
 
     def best_copy(g, j):
         return pltpu.make_async_remote_copy(
@@ -281,7 +302,6 @@
                 best_copy(g, j).start()
 
     width = best.shape[2]
-    own_tokens = tokens // n_patches
     column = lax.broadcasted_iota(jnp.int32, (send.shape[1], width), 1)
     query = lax.broadcasted_iota(jnp.int32, (send.shape[1], width), 0)
     position = column // own_tokens
@@ -314,7 +334,7 @@
         total = best[g]
         for k in range(1, n_patches):
             total = jnp.maximum(total, best_in[g, lax.rem(me_j + k, n_patches)])
-        send[g, :, :pairs] = mean_of(total)
+        send[g, :, :packed] = mean_of(total)
         score_copy(g, 1).start()
 
         @pl.when(g == me_p)
@@ -419,18 +439,17 @@
 
     drain_maxima()
     cands = cand_ref.shape[1]
-    spots = lax.broadcasted_iota(jnp.int32, (cands, pairs), 1)
-    zeros = tuple(jnp.zeros((cands, pairs), jnp.float32) for _ in range(nq))
+    spots = lax.broadcasted_iota(jnp.int32, (cands, packed), 1)
+    zeros = tuple(jnp.zeros((cands, packed), jnp.float32) for _ in range(nq))
 
     def pick(h, scores, picked):
         found = []
         for q in range(nq):
             mine = key[q * cands : (q + 1) * cands]
             total = picked[q]
-            for half in range(2):
-                spot = (spots + (h * lanes + half * pairs)).astype(jnp.float32)
-                line = scores[half * nq + q : half * nq + q + 1, :]
-                total = total + jnp.where(mine == spot, line, 0.0)
+            for kind in range(2 * nq):
+                spot = (spots + (h * lanes + kind * packed)).astype(jnp.float32)
+                total = total + jnp.where(mine == spot, scores[kind : kind + 1, :], 0.0)
             found.append(total)
         return tuple(found)
 
@@ -455,7 +474,7 @@
             wait_scores(me_p)
 
         def scores_of(h):
-            return arrived[h, :, :pairs]
+            return arrived[h, :, :packed]
 
         def later(k, picked):
             h = holder(n_pages - 2 - k)
@@ -467,25 +486,25 @@
     @pl.when(direct)
     def _():
         key_rows = [to_row(key[q * cands : (q + 1) * cands]) for q in range(nq)]
-        slot = lax.broadcasted_iota(jnp.int32, (pairs, cands), 0)
-        lane_of = lax.broadcasted_iota(jnp.int32, (pairs, width), 1) // own_tokens
-        kind = lane_of // (n_patches * nq) * nq + lane_of % nq
+        slot = lax.broadcasted_iota(jnp.int32, (packed, cands), 0)
+        lane_of = lax.broadcasted_iota(jnp.int32, (packed, width), 1) // own_tokens
+        kind_of = lane_of // (n_patches * nq) * nq + lane_of % nq
 
         def hits(h):
-            return [
-                (slot + (h * lanes + half * pairs)).astype(jnp.float32) == key_rows[q]
-                for half in range(2)
-                for q in range(nq)
+            spots = [
+                (slot + (h * lanes + kind * packed)).astype(jnp.float32) for kind in range(2 * nq)
             ]
+            return [[spot == key_row for key_row in key_rows] for spot in spots]
 
         def add(hit, total, sums):
             sums = list(sums)
-            for k in range(2 * nq):
-                score = jnp.sum(jnp.where(kind == k, total, 0.0), axis=1, keepdims=True)
-                sums[k % nq] = sums[k % nq] + jnp.where(hit[k], score, 0.0)
+            for kind in range(2 * nq):
+                score = jnp.sum(jnp.where(kind_of == kind, total, 0.0), axis=1, keepdims=True)
+                for q in range(nq):
+                    sums[q] = sums[q] + jnp.where(hit[kind][q], score, 0.0)
             return tuple(sums)
 
-        sums = tuple(jnp.zeros((pairs, cands), jnp.float32) for _ in range(nq))
+        sums = tuple(jnp.zeros((packed, cands), jnp.float32) for _ in range(nq))
         wait(direct_in.at[0, pl.ds(0, n_patches - 1)], d_in.at[0])
         total = best[0]
         for k in range(1, n_patches):
@@ -512,8 +531,8 @@
     nq, own_tokens, dim = queries.shape
     n_pages, n_patches = lax.axis_size("pages"), lax.axis_size("patches")
     most = 3 * nq * candidates.shape[1] // n_pages
-    pairs = up(up(most, 2) // 2, 8)
-    lanes = up(2 * pairs, 128)
+    packed = -(-most // (2 * nq))
+    lanes = up(2 * nq * packed, 128)
     width = 2 * n_patches * nq * own_tokens
     vmem = pl.BlockSpec(memory_space=pltpu.VMEM)
     dma = pltpu.SemaphoreType.DMA
@@ -530,9 +549,9 @@
             pltpu.VMEM(gallery.shape, jnp.bfloat16),
             pltpu.VMEM((n_pages, 1, lanes), jnp.int32),
             pltpu.SMEM((n_pages, 1, lanes), jnp.int32),
-            pltpu.VMEM((n_pages, pairs, width), jnp.float32),
-            pltpu.VMEM((n_pages, n_patches, pairs, width), jnp.float32),
-            pltpu.VMEM((n_pages, n_patches, pairs, width), jnp.float32),
+            pltpu.VMEM((n_pages, packed, width), jnp.float32),
+            pltpu.VMEM((n_pages, n_patches, packed, width), jnp.float32),
+            pltpu.VMEM((n_pages, n_patches, packed, width), jnp.float32),
             pltpu.VMEM((n_pages, up(2 * nq, 8), lanes), jnp.float32),
             pltpu.VMEM((n_pages, up(2 * nq, 8), lanes), jnp.float32),
             dma,

time: 16.6 us -> 16.7 us (level)
  no operation moved by 1% of the time
where the time goes in v4:
time: 16.7 us; the launch traced here: 16.5 us
  Pallas kernels  15.9 us (95%)
  local copies, waits for them, and re-layouts  0.56 us (3%)
    pallas_call x1, Pallas kernels, body(): pl.pallas_call(functools.partial(kernel, (n_pages, n_patches, nq, own_tok...  15.9 us
    unnamed x1, local copies, waits for them, and re-layouts  0.56 us

profile of v4, /device:TPU:0, one launch (start us, length us, event | category | flops | bytes accessed | tf_op | source)
XLA Modules:
  0.0 16.5 jit_solution(4334878991982480586)
XLA Ops:
  0.0 15.9 %shard_map.46 = f32[2,32]{1,0:T(2,128)S(1)} custom-call(bf16[16,128]{1,0:T(8,128)(2,1)} %bitcast.1, bf16[80,256,128]{2,1,0:T(8,128)(2,1)} %g_ref.1, s32[320]{0:T(512)} %rows_hbm.1, s32[2,32]{1,0:T(2,128)} %cand_hbm.1), custom_call_target="tpu_custom_call" | custom-call | tf_op jit(solution)/shard_map/pallas_call | solution.py:539
  16.0 0.6 %copy.6 = f32[2,32]{1,0:T(2,128)} copy(f32[2,32]{1,0:T(2,128)S(1)} %shard_map.46) | data formatting | bytes 512
